TPU v7x, 32 devices: a whole 2x2x4 slice. The times are simulated.
32 devices in a mesh: gx: 4 (over x, core), gy: 8 (over z, y).
Axes of the slice: x: 2, y: 2, z: 4, core: 2. Of those that a mesh axis runs over, the one named last changes fastest.
Arguments:
- base: int32 [2, 3, 65536], P(None, None, ('gx', 'gy')), may hold values from -2 to 125, as said below
- offset: float32 [2, 3, 65536], P(None, None, ('gx', 'gy')), may hold values from 0.5 to 1.5
- velocity: float32 [3, 65536], P(None, ('gx', 'gy')), may hold values from -4 to 4
- affine: float32 [9, 65536], P(None, ('gx', 'gy')), may hold values from -3 to 3
- volume: float32 [65536], P(('gx', 'gy')), may hold values from 0.8 to 1.25
- node_mask: int32 [128, 128, 128], P('gx', 'gy'), may hold values 0 or 1
- direction: int32 [65536], P(('gx', 'gy')), may hold values from 0 to 8, as said below
Outputs:
- migrated: float32 [16, 98304], P(None, ('gx', 'gy'))
Inputs may be any that keep to these rules, and one draw needn't show every extreme that they name: base[s, 0] lies in -2 to 31, base[s, 1] in -2 to 15, base[s, 2] in 0 to 125. Of one block column's rows, at most 128 carry any one direction other than 4; in every draw some block column has exactly 128 rows in some direction.
All inputs are finite; a program needn't handle non-finite values. No bound on the sum of `node_mask` on one device may be relied on, other than what follows from the above.
Results may differ from a plain program's by a relative error of at most 0.0003.
Values may be sent and summed in bfloat16 or wider, within the bound.
A program may use at most 64 MiB of HBM per device.

v0:
```python
import functools

import jax
import jax.numpy as jnp
import numpy as np
from jax import lax
from jax.experimental import pallas as pl
from jax.experimental.pallas import tpu as pltpu
from jax.sharding import PartitionSpec as P

PARTICLE_MASS = 1.0
STIFFNESS = 4.0
TIME_STEP = 0.1
GRAVITY = 3.0
MASS_FLOOR = 0.5
LANES = 128
OUTSIDE = -100

F32 = jnp.float32
BF16 = jnp.bfloat16
NT = (((1,), (1,)), ((), ()))

BLOCKS = ((0, -1), (0, 1), (-1, 0), (1, 0), (-1, -1), (-1, 1), (1, -1), (1, 1))
CORNER_ROWS = 16


def block_rows(size_x, size_y):
    counts = [2 * size_x] * 2 + [2 * size_y] * 2 + [CORNER_ROWS] * 4
    starts = [sum(counts[:place]) for place in range(8)]
    return (list(zip(starts, counts)), sum(counts))


def owner_rows(size_x, size_y):
    places, total = block_rows(size_x, size_y)
    rows = np.full(total, -1, np.int64)
    for (dx, dy), (start, _) in zip(BLOCKS, places):
        span_x = range(2) if dx else range(size_x)
        span_y = range(2) if dy else range(size_y)
        low_x = size_x - 2 if dx < 0 else 0
        low_y = size_y - 2 if dy < 0 else 0
        for x in span_x:
            for y in span_y:
                if dx and dy:
                    spot = 2 * x + y
                elif dx:
                    spot = x * size_y + y
                else:
                    spot = y * size_x + x
                rows[start + spot] = (low_x + x) * size_y + low_y + y
    return rows


def spline(frac):
    return [0.5 * (1.5 - frac) ** 2, 0.75 - (frac - 1.0) ** 2, 0.5 * (frac - 0.5) ** 2]


def pick(place, values):
    return jnp.where(
        place == 0,
        values[0],
        jnp.where(place == 1, values[1], jnp.where(place == 2, values[2], 0.0)),
    )


def weights_of(offsets):
    weights = [spline(offsets[axis : axis + 1]) for axis in range(3)]
    slopes = [
        [weights[axis][node] * (float(node) - offsets[axis : axis + 1]) for node in range(3)]
        for axis in range(3)
    ]
    return (weights, slopes)


def rows_iota(count):
    return lax.broadcasted_iota(jnp.int32, (count, 1), 0)


def build(bases, weights, slopes, size_x, size_y, tab, xw, xs, yw, ys):
    width = bases.shape[1]
    from_x = bases[0:1] + 2
    from_y = bases[1:2] + 2
    edge = rows_iota(8)
    for size, start, axis, plain, slope in ((size_x, from_x, 0, xw, xs), (size_y, from_y, 1, yw, ys)):
        place = rows_iota(size) + 2 - start
        plain[0:size] = pick(place, weights[axis])
        slope[0:size] = pick(place, slopes[axis])
        coord = jnp.where(edge < 2, edge, jnp.where(edge < 4, edge + size, OUTSIDE))
        place = coord - start
        plain[size : size + 8] = pick(place, weights[axis])
        slope[size : size + 8] = pick(place, slopes[axis])

    def put(row, count, wx, sx, wy, sy):
        tab[row : row + count, 0:width] = (wx * wy).astype(BF16)
        tab[row : row + count, width : 2 * width] = (sx * wy).astype(BF16)
        tab[row : row + count, 2 * width : 3 * width] = (wx * sy).astype(BF16)

    places, margin = block_rows(size_x, size_y)
    wide_w, wide_s = (xw[0:size_x], xs[0:size_x])
    for k in range(4):
        one = slice(size_y + k, size_y + k + 1)
        put(k * size_x, size_x, wide_w, wide_s, yw[one], ys[one])
    tall_w, tall_s = (yw[0:size_y], ys[0:size_y])
    for k in range(4):
        one = slice(size_x + k, size_x + k + 1)
        put(places[2][0] + k * size_y, size_y, xw[one], xs[one], tall_w, tall_s)
    spot = rows_iota(CORNER_ROWS)
    for k in range(4):
        high_x, high_y = (k // 2, k % 2)
        coord_x = jnp.where(spot < 4, (spot >> 1) + high_x * (size_x + 2), OUTSIDE)
        coord_y = jnp.where(spot < 4, (spot & 1) + high_y * (size_y + 2), OUTSIDE)
        place_x = coord_x - from_x
        place_y = coord_y - from_y
        put(
            places[4 + k][0],
            CORNER_ROWS,
            pick(place_x, weights[0]),
            pick(place_x, slopes[0]),
            pick(place_y, weights[1]),
            pick(place_y, slopes[1]),
        )
    for x in range(size_x):
        one = slice(x, x + 1)
        put(margin + x * size_y, size_y, xw[one], xs[one], tall_w, tall_s)


def depth_tables(bases, weights, slopes, depth):
    place = rows_iota(depth) - bases[2:3]
    return (pick(place, weights[2]), pick(place, slopes[2]))


def scatter_chunk(bases, offsets, vel, aff, vol, sizes, tab, right, tables, total):
    size_x, size_y, depth = sizes
    width = bases.shape[1]
    weights, slopes = weights_of(offsets)
    build(bases, weights, slopes, size_x, size_y, tab, *tables)
    depth_w, depth_s = depth_tables(bases, weights, slopes, depth)
    stress = -STIFFNESS * (vol - 1.0)

    def entry(i, j):
        value = PARTICLE_MASS * aff[3 * i + j]
        return value + stress if i == j else value

    zeros = jnp.zeros((depth, 2 * width), BF16)
    right[0:depth, 0:width] = (depth_w * PARTICLE_MASS).astype(BF16)
    right[0:depth, width : 3 * width] = zeros
    for i in range(3):
        rows = slice((i + 1) * depth, (i + 2) * depth)
        moment = PARTICLE_MASS * vel[i]
        right[rows, 0:width] = (depth_w * moment + depth_s * entry(i, 2)).astype(BF16)
        right[rows, width : 2 * width] = (depth_w * entry(i, 0)).astype(BF16)
        right[rows, 2 * width : 3 * width] = (depth_w * entry(i, 1)).astype(BF16)
    total[...] += lax.dot_general(tab[...], right[...], NT, preferred_element_type=F32)


def gather_chunk(bases, offsets, vol, sizes, wide, tab, result, tables):
    size_x, size_y, depth = sizes
    width = bases.shape[1]
    weights, slopes = weights_of(offsets)
    build(bases, weights, slopes, size_x, size_y, tab, *tables)
    depth_w, depth_s = depth_tables(bases, weights, slopes, depth)
    result[...] = jnp.dot(wide[...], tab[...], preferred_element_type=F32)
    vel, aff = ([], [None] * 9)
    for i in range(3):
        rows = slice(i * depth, (i + 1) * depth)
        plain = result[rows, 0:width]
        vel.append(jnp.sum(plain * depth_w, 0, keepdims=True))
        aff[3 * i + 2] = 4.0 * jnp.sum(plain * depth_s, 0, keepdims=True)
        aff[3 * i] = 4.0 * jnp.sum(result[rows, width : 2 * width] * depth_w, 0, keepdims=True)
        aff[3 * i + 1] = 4.0 * jnp.sum(
            result[rows, 2 * width : 3 * width] * depth_w, 0, keepdims=True
        )
    vol = vol * (1.0 + TIME_STEP * (aff[0] + aff[4] + aff[8]))
    return (vel, aff, vol)


def take_rows(ref, lanes, count):
    return [ref[k : k + 1, lanes] for k in range(count)]


def first_kernel(sizes, chunk, base, offset, vel, aff, vol, core, margins, tab, right, total, *tables):
    total[...] = jnp.zeros_like(total)

    def body(step, carry):
        lanes = pl.ds(pl.multiple_of(step * chunk, chunk), chunk)
        scatter_chunk(
            base[0, :, lanes], offset[0, :, lanes], take_rows(vel, lanes, 3),
            take_rows(aff, lanes, 9), vol[:, lanes], sizes, tab, right, tables, total,
        )
        return carry

    lax.fori_loop(0, vel.shape[1] // chunk, body, 0)
    edge = margins.shape[0]
    margins[...] = total[0:edge].astype(BF16)
    core[...] = total[edge:]


def middle_kernel(sizes, chunk, base, offset, vol, wide, core, margins, vol_out, tab, result, right, total, *tables):
    total[...] = jnp.zeros_like(total)

    def body(step, carry):
        lanes = pl.ds(pl.multiple_of(step * chunk, chunk), chunk)
        vel, aff, ratio = gather_chunk(
            base[0, :, lanes], offset[0, :, lanes], vol[:, lanes], sizes, wide, tab, result, tables
        )
        vol_out[:, lanes] = ratio
        scatter_chunk(
            base[1, :, lanes], offset[1, :, lanes], vel, aff, ratio, sizes, tab, right, tables, total
        )
        return carry

    lax.fori_loop(0, vol.shape[1] // chunk, body, 0)
    edge = margins.shape[0]
    margins[...] = total[0:edge].astype(BF16)
    core[...] = total[edge:]


def last_kernel(sizes, chunk, capacity, counts, base, offset, vol, wide, direction, own, buckets, tab, result, state, slots, *tables):
    size_x, size_y, _ = sizes
    count_x, count_y = counts
    index_x = lax.axis_index("gx")
    index_y = lax.axis_index("gy")
    rows = vol.shape[1]

    def route(code):
        step_x = jnp.where(code < 3, -1, jnp.where(code > 5, 1, 0))
        step_y = code - 3 * step_x - 4
        to_x = step_x + index_x
        to_y = step_y + index_y
        inside = (to_x >= 0) & (to_x < count_x) & (to_y >= 0) & (to_y < count_y)
        return (
            jnp.where(inside, code, 4),
            jnp.where(inside, step_x, 0),
            jnp.where(inside, step_y, 0),
        )

    def body(step, carry):
        lanes = pl.ds(pl.multiple_of(step * chunk, chunk), chunk)
        bases = base[1, :, lanes]
        offsets = offset[1, :, lanes]
        vel, aff, ratio = gather_chunk(
            bases, offsets, vol[:, lanes], sizes, wide, tab, result, tables
        )
        moving, step_x, step_y = route(direction[:, lanes])
        shift = (step_x * size_x, step_y * size_y, None)
        for axis in range(3):
            spot = bases[axis : axis + 1].astype(F32) + offsets[axis : axis + 1]
            spot = spot + TIME_STEP * vel[axis]
            if shift[axis] is not None:
                spot = spot - shift[axis].astype(F32)
            state[axis : axis + 1, lanes] = spot
            state[3 + axis : 4 + axis, lanes] = vel[axis]
        for k in range(9):
            state[6 + k : 7 + k, lanes] = aff[k]
        state[15:16, lanes] = ratio
        own[:, lanes] = jnp.where(moving == 4, state[:, lanes], 0.0)
        return carry

    lax.fori_loop(0, rows // chunk, body, 0)

    parts = rows // LANES
    place = rows_iota(8)
    codes = jnp.where(place < 4, place, place + 1)
    hits = []
    for part in range(parts):
        moving, _, _ = route(direction[:, part * LANES : (part + 1) * LANES])
        hits.append(jnp.where(moving == codes, 1.0, 0.0))
    above = lax.broadcasted_iota(jnp.int32, (LANES, 2 * LANES), 0)
    along = lax.broadcasted_iota(jnp.int32, (LANES, 2 * LANES), 1)
    summer = jnp.where(above <= along, 1.0, 0.0).astype(BF16)
    sums = jnp.dot(jnp.concatenate(hits, 0).astype(BF16), summer, preferred_element_type=F32)
    before = (place * capacity).astype(F32)
    before = jnp.broadcast_to(before, (8, LANES))
    for part in range(parts):
        mine = slice(part * 8, (part + 1) * 8)
        slot = jnp.sum(hits[part] * (sums[mine, 0:LANES] + before), 0, keepdims=True) - 1.0
        slots[:, part * LANES : (part + 1) * LANES] = slot.astype(jnp.int32)
        before = before + sums[mine, LANES:]

    value = state[...]
    high = value.astype(BF16)
    rest = value - high.astype(F32)
    middle = rest.astype(BF16)
    low = (rest - middle.astype(F32)).astype(BF16)
    split = jnp.concatenate([high, middle, low], 0)
    for k in range(8):
        chosen = slots[...] - k * capacity == rows_iota(capacity)
        chosen = jnp.where(chosen, 1.0, 0.0).astype(BF16)
        packed = lax.dot_general(split, chosen, NT, preferred_element_type=F32)
        buckets[k] = packed[0:16] + packed[16:32] + packed[32:48]


def neighbour(counts, dx, dy):
    to_x = lax.axis_index("gx") + dx
    to_y = lax.axis_index("gy") + dy
    exists = (to_x >= 0) & (to_x < counts[0]) & (to_y >= 0) & (to_y < counts[1])
    return (exists, {"gx": to_x, "gy": to_y})


def greet(counts):
    barrier = pltpu.get_barrier_semaphore()
    for dx, dy in BLOCKS:
        exists, where = neighbour(counts, dx, dy)

        @pl.when(exists)
        def _():
            pl.semaphore_signal(
                barrier, inc=1, device_id=where, device_id_type=pl.DeviceIdType.MESH
            )

    peers = 0
    for dx, dy in BLOCKS:
        exists, _ = neighbour(counts, dx, dy)
        peers = peers + exists.astype(jnp.int32)
    pl.semaphore_wait(barrier, peers)


def transfers(counts, sign, views, source, target, send_sems, recv_sems):
    copies = []
    for k, (dx, dy) in enumerate(BLOCKS):
        exists, where = neighbour(counts, sign * dx, sign * dy)
        copy = pltpu.make_async_remote_copy(
            src_ref=views(source, k),
            dst_ref=views(target, k),
            send_sem=send_sems.at[k],
            recv_sem=recv_sems.at[k],
            device_id=where,
            device_id_type=pl.DeviceIdType.MESH,
        )
        comes, _ = neighbour(counts, -sign * dx, -sign * dy)
        copies.append((exists, comes, copy))
    return copies


def start_all(copies, views, target):
    for exists, _, copy in copies:
        pl.when(exists)(copy.start)
    for k, (_, comes, _) in enumerate(copies):

        @pl.when(jnp.logical_not(comes))
        def _():
            view = views(target, k)
            view[...] = jnp.zeros(view.shape, view.dtype)


def wait_all(copies):
    for exists, comes, copy in copies:
        pl.when(comes)(copy.wait_recv)
    for exists, comes, copy in copies:
        pl.when(exists)(copy.wait_send)


def grid_kernel(sizes, counts, core, margins, mask, place_in, take_out, wide, got, sent, halo, speed, sends, recvs, sends_b, recvs_b):
    size_x, size_y, depth = sizes
    places, edge = block_rows(size_x, size_y)

    def views(ref, k):
        return ref.at[pl.ds(places[k][0], places[k][1])]

    greet(counts)
    copies = transfers(counts, 1, views, margins, got, sends, recvs)
    start_all(copies, views, got)
    wait_all(copies)
    total = core[...] + jnp.dot(place_in[...], got[...], preferred_element_type=F32)
    mass = jnp.maximum(total[:, 0:depth], MASS_FLOOR)
    keep = (1 - mask[...]).astype(F32)
    for axis in range(3):
        value = total[:, (axis + 1) * depth : (axis + 2) * depth] / mass
        if axis == 2:
            value = value - TIME_STEP * GRAVITY
        speed[:, axis * depth : (axis + 1) * depth] = (value * keep).astype(BF16)
    sent[...] = jnp.dot(take_out[...], speed[...], preferred_element_type=F32).astype(BF16)
    copies = transfers(counts, -1, views, sent, halo, sends_b, recvs_b)
    start_all(copies, views, halo)
    for axis in range(3):
        lanes = slice(axis * depth, (axis + 1) * depth)
        wide[lanes, edge:] = speed[:, lanes].astype(F32).T.astype(BF16)
    wait_all(copies)
    for axis in range(3):
        lanes = slice(axis * depth, (axis + 1) * depth)
        wide[lanes, 0:edge] = halo[:, lanes].astype(F32).T.astype(BF16)


def migrate_kernel(counts, buckets, out, got, sends, recvs):
    capacity = buckets.shape[2]
    order = [0, 1, 2, 3, 5, 6, 7, 8]
    slot_of = [order.index(3 * (dx + 1) + dy + 1) for dx, dy in BLOCKS]

    def views(ref, k):
        return ref.at[slot_of[k]]

    greet(counts)
    copies = transfers(counts, 1, views, buckets, got, sends, recvs)
    start_all(copies, views, got)
    wait_all(copies)
    for k in range(8):
        out[:, k * capacity : (k + 1) * capacity] = got[k]


def vmem(count):
    return [pl.BlockSpec(memory_space=pltpu.VMEM)] * count


def per_device(counts, base, offset, velocity, affine, volume, node_mask, direction):
    sizes = node_mask.shape
    size_x, size_y, depth = sizes
    rows = velocity.shape[1]
    capacity = rows // 16
    chunk = min(rows, 512)
    _, edge = block_rows(size_x, size_y)
    cells = size_x * size_y
    all_rows = edge + cells
    volume = volume.reshape(1, rows)
    direction = direction.reshape(1, rows)
    mask = node_mask.reshape(cells, depth)
    owners = owner_rows(size_x, size_y)
    choose = (owners[:, None] == np.arange(cells)[None]).astype(np.float32)
    take_out = jnp.asarray(choose, BF16)
    place_in = jnp.asarray(choose.T, BF16)

    tab = pltpu.VMEM((all_rows, 3 * chunk), BF16)
    right = pltpu.VMEM((4 * depth, 3 * chunk), BF16)
    result = pltpu.VMEM((3 * depth, 3 * chunk), F32)
    total = pltpu.VMEM((all_rows, 4 * depth), F32)
    tables = [pltpu.VMEM((size_x + 8, chunk), F32)] * 2 + [pltpu.VMEM((size_y + 8, chunk), F32)] * 2
    grid_out = [
        jax.ShapeDtypeStruct((cells, 4 * depth), F32),
        jax.ShapeDtypeStruct((edge, 4 * depth), BF16),
    ]
    params = pltpu.CompilerParams(vmem_limit_bytes=56 * 1024 * 1024)

    core, margins = pl.pallas_call(
        functools.partial(first_kernel, sizes, chunk),
        out_shape=grid_out,
        in_specs=vmem(5),
        out_specs=vmem(2),
        scratch_shapes=[tab, right, total] + tables,
        compiler_params=params,
        name="scatter",
    )(base, offset, velocity, affine, volume)

    def exchange(core, margins):
        return pl.pallas_call(
            functools.partial(grid_kernel, sizes, counts),
            out_shape=jax.ShapeDtypeStruct((3 * depth, all_rows), BF16),
            in_specs=vmem(5),
            out_specs=vmem(1)[0],
            scratch_shapes=[
                pltpu.VMEM((edge, 4 * depth), BF16),
                pltpu.VMEM((edge, 3 * depth), BF16),
                pltpu.VMEM((edge, 3 * depth), BF16),
                pltpu.VMEM((cells, 3 * depth), BF16),
            ]
            + [pltpu.SemaphoreType.DMA((8,))] * 4,
            compiler_params=pltpu.CompilerParams(
                collective_id=0, has_side_effects=True, vmem_limit_bytes=56 * 1024 * 1024
            ),
            name="exchange",
        )(core, margins, mask, place_in, take_out)

    wide = exchange(core, margins)
    core, margins, volume = pl.pallas_call(
        functools.partial(middle_kernel, sizes, chunk),
        out_shape=grid_out + [jax.ShapeDtypeStruct((1, rows), F32)],
        in_specs=vmem(4),
        out_specs=vmem(3),
        scratch_shapes=[tab, result, right, total] + tables,
        compiler_params=params,
        name="gather_scatter",
    )(base, offset, volume, wide)
    wide = exchange(core, margins)
    own, buckets = pl.pallas_call(
        functools.partial(last_kernel, sizes, chunk, capacity, counts),
        out_shape=[
            jax.ShapeDtypeStruct((16, rows), F32),
            jax.ShapeDtypeStruct((8, 16, capacity), F32),
        ],
        in_specs=vmem(5),
        out_specs=vmem(2),
        scratch_shapes=[tab, result, pltpu.VMEM((16, rows), F32), pltpu.VMEM((1, rows), jnp.int32)]
        + tables,
        compiler_params=params,
        name="gather_pack",
    )(base, offset, volume, wide, direction)
    arrived = pl.pallas_call(
        functools.partial(migrate_kernel, counts),
        out_shape=jax.ShapeDtypeStruct((16, 8 * capacity), F32),
        in_specs=vmem(1),
        out_specs=vmem(1)[0],
        scratch_shapes=[pltpu.VMEM((8, 16, capacity), F32)] + [pltpu.SemaphoreType.DMA((8,))] * 2,
        compiler_params=pltpu.CompilerParams(collective_id=1, has_side_effects=True),
        name="migrate",
    )(buckets)
    return jnp.concatenate([own, arrived], 1)


def solution(mesh):
    counts = (mesh.shape["gx"], mesh.shape["gy"])
    placed = (
        P(None, None, ("gx", "gy")),
        P(None, None, ("gx", "gy")),
        P(None, ("gx", "gy")),
        P(None, ("gx", "gy")),
        P(("gx", "gy")),
        P("gx", "gy", None),
        P(("gx", "gy")),
    )
    return jax.shard_map(
        functools.partial(per_device, counts),
        mesh=mesh,
        in_specs=placed,
        out_specs=P(None, ("gx", "gy")),
        check_vma=False,
    )
```

profile of v0, /device:TPU:0, one launch (start us, length us, event | category | flops | bytes accessed | tf_op | source)
XLA Modules:
  0.0 72.4 jit_solution(6066251035588414178)
XLA Ops:
  0.0 0.0 copy-start.1
  0.0 1.5 %copy.14.base = s32[2,3,2048]{2,1,0:T(4,128)} copy(s32[2,3,2048]{2,0,1:T(2,128)} %param.9) | data formatting | bytes 98304 | tf_op args[0]
  1.5 0.0 copy-done.1
  1.5 0.7 copy.15.offset
  2.1 8.2 %scatter.1 = (f32[512,512]{1,0:T(8,128)}, bf16[256,512]{1,0:T(8,128)(2,1)}) custom-call(s32[2,3,2048]{2,1,0:T(4,128)} %copy.14.base, f32[2,3,2048]{2,1,0:T(4,128)} %copy.15.offset, f32[3,2048]{1,0:T(4,128)} %vel.1, f32[9,2048]{1,0:T(8,128)} %aff.1, f32[1,2048]{1,0:T(1,128)} %bitcast.5), custom_call_target="tpu_custom_call" | custom-call | tf_op jit(solution)/shard_map/scatter/pallas_call | solution.py:431
  10.3 15.8 %exchange.2.wide = bf16[384,768]{1,0:T(8,128)(2,1)} custom-call(f32[512,512]{1,0:T(8,128)} %get-tuple-element.12.core, bf16[256,512]{1,0:T(8,128)(2,1)} %get-tuple-element.13.margins, s32[512,128]{1,0:T(8,128)} %bitcast.3, bf16[512,256]{1,0:T(8,128)(2,1)} %constant.5.clone.place_in, bf16[256,512]{1,0:T(8,128)(2,1)} %constant.4.clone.take_out), custom_call_target="tpu_custom_call" | custom-call | tf_op jit(solution)/shard_map/exchange/pallas_call | solution.py:442
  26.1 13.2 %gather_scatter.1 = (f32[512,512]{1,0:T(8,128)}, bf16[256,512]{1,0:T(8,128)(2,1)}, f32[1,2048]{1,0:T(1,128)}) custom-call(s32[2,3,2048]{2,1,0:T(4,128)} %copy.14.base, f32[2,3,2048]{2,1,0:T(4,128)} %copy.15.offset, f32[1,2048]{1,0:T(1,128)} %bitcast.6, bf16[384,768]{1,0:T(8,128)(2,1)} %exchange.2.wide), custom_call_target="tpu_custom_call" | custom-call | tf_op jit(solution)/shard_map/gather_scatter/pallas_call | solution.py:461
  39.3 15.2 %exchange.3.wide = bf16[384,768]{1,0:T(8,128)(2,1)} custom-call(f32[512,512]{1,0:T(8,128)} %get-tuple-element.15.core, bf16[256,512]{1,0:T(8,128)(2,1)} %get-tuple-element.16.margins, s32[512,128]{1,0:T(8,128)} %bitcast.4, bf16[512,256]{1,0:T(8,128)(2,1)} %constant.5.clone.place_in, bf16[256,512]{1,0:T(8,128)(2,1)} %constant.4.clone.take_out), custom_call_target="tpu_custom_call" | custom-call | tf_op jit(solution)/shard_map/exchange/pallas_call | solution.py:442
  54.5 8.5 %gather_pack.1 = (f32[16,2048]{1,0:T(8,128)}, f32[8,16,128]{2,1,0:T(8,128)}) custom-call(s32[2,3,2048]{2,1,0:T(4,128)} %copy.14.base, f32[2,3,2048]{2,1,0:T(4,128)} %copy.15.offset, f32[1,2048]{1,0:T(1,128)} %get-tuple-element.14.vol, bf16[384,768]{1,0:T(8,128)(2,1)} %exchange.3.wide, s32[1,2048]{1,0:T(1,128)} %bitcast.7), custom_call_target="tpu_custom_call" | custom-call | tf_op jit(solution)/shard_map/gather_pack/pallas_call | solution.py:471
  63.0 0.0 copy-start
  63.0 7.8 %migrate.1 = f32[16,1024]{1,0:T(8,128)} custom-call(f32[8,16,128]{2,1,0:T(8,128)} %get-tuple-element.18.buckets), custom_call_target="tpu_custom_call" | custom-call | tf_op jit(solution)/shard_map/migrate/pallas_call | solution.py:484
  70.8 0.0 copy-done
  70.8 1.5 %pad_maximum_fusion = f32[16,3072]{1,0:T(8,128)} fusion(f32[16,1024]{1,0:T(8,128)} %migrate.1, f32[16,2048]{1,0:T(8,128)S(1)} %copy-done), kind=kLoop, calls=%fused_computation | loop fusion | flops 49152 | bytes 393216 | tf_op jit(solution)/shard_map/concatenate | solution.py:493
Async XLA Ops:
  0.0 1.5 %copy-start.1 = (f32[2,3,2048]{2,0,1:T(2,128)S(1)}, f32[2,3,2048]{2,0,1:T(2,128)}, u32[]{:S(2)}) copy-start(f32[2,3,2048]{2,0,1:T(2,128)} %param.10) | copy-start | bytes 147460
  63.0 7.8 %copy-start = (f32[16,2048]{1,0:T(8,128)S(1)}, f32[16,2048]{1,0:T(8,128)}, u32[]{:S(2)}) copy-start(f32[16,2048]{1,0:T(8,128)} %get-tuple-element.17) | copy-start | bytes 393220
where the time goes:
time: 72.8 us; the launch traced here: 72.4 us
  Pallas kernels  68.7 us (94%)
  local copies, waits for them, and re-layouts  2.12 us (3%)
  other arithmetic  1.53 us (2%)
    pallas_call x2, Pallas kernels, exchange(): pl.pallas_call(functools.partial(grid_kernel, sizes, counts), out_shape=j...  31.1 us
    pallas_call x1, Pallas kernels, per_device(): pl.pallas_call(functools.partial(middle_kernel, sizes, chunk), out_shape=...  13.2 us
    pallas_call x1, Pallas kernels, per_device(): pl.pallas_call(functools.partial(last_kernel, sizes, chunk, capacity, cou...  8.49 us
    pallas_call x1, Pallas kernels, per_device(): pl.pallas_call(functools.partial(first_kernel, sizes, chunk), out_shape=g...  8.16 us
    pallas_call x1, Pallas kernels, per_device(): pl.pallas_call(functools.partial(migrate_kernel, counts), out_shape=jax.S...  7.78 us
    unnamed x6, local copies, waits for them, and re-layouts  2.12 us
    concatenate x1, other arithmetic, per_device(): return jnp.concatenate([own, arrived], 1)  1.53 us

commit v1 on v0

--- a/solution.py
+++ b/solution.py
@@ -130,6 +130,7 @@
 
 def scatter_chunk(bases, offsets, vel, aff, vol, sizes, tab, right, tables, total):
     size_x, size_y, depth = sizes
+    _, edge = block_rows(size_x, size_y)
     width = bases.shape[1]
     weights, slopes = weights_of(offsets)
     build(bases, weights, slopes, size_x, size_y, tab, *tables)
@@ -149,7 +150,7 @@
         right[rows, 0:width] = (depth_w * moment + depth_s * entry(i, 2)).astype(BF16)
         right[rows, width : 2 * width] = (depth_w * entry(i, 0)).astype(BF16)
         right[rows, 2 * width : 3 * width] = (depth_w * entry(i, 1)).astype(BF16)
-    total[...] += lax.dot_general(tab[...], right[...], NT, preferred_element_type=F32)
+    total[0:edge] += lax.dot_general(tab[0:edge], right[...], NT, preferred_element_type=F32)
 
 
 def gather_chunk(bases, offsets, vol, sizes, wide, tab, result, tables):
@@ -177,44 +178,47 @@
     return [ref[k : k + 1, lanes] for k in range(count)]
 
 
-def first_kernel(sizes, chunk, base, offset, vel, aff, vol, core, margins, tab, right, total, *tables):
+def first_kernel(sizes, counts, chunk, base, offset, vel, aff, vol, mask, place_in, take_out, wide, tab, right, total, xw, xs, yw, ys, *remote):
+    greet(counts)
     total[...] = jnp.zeros_like(total)
 
     def body(step, carry):
         lanes = pl.ds(pl.multiple_of(step * chunk, chunk), chunk)
         scatter_chunk(
             base[0, :, lanes], offset[0, :, lanes], take_rows(vel, lanes, 3),
-            take_rows(aff, lanes, 9), vol[:, lanes], sizes, tab, right, tables, total,
+            take_rows(aff, lanes, 9), vol[:, lanes], sizes, tab.at[step], right.at[step],
+            (xw, xs, yw, ys), total,
         )
         return carry
 
     lax.fori_loop(0, vel.shape[1] // chunk, body, 0)
-    edge = margins.shape[0]
-    margins[...] = total[0:edge].astype(BF16)
-    core[...] = total[edge:]
-
-
-def middle_kernel(sizes, chunk, base, offset, vol, wide, core, margins, vol_out, tab, result, right, total, *tables):
+    exchange(sizes, counts, mask, place_in, take_out, wide, tab, right, total, *remote)
+
+
+def middle_kernel(sizes, counts, chunk, base, offset, vol, before, mask, place_in, take_out, wide, vol_out, seen, result, tab, right, total, xw, xs, yw, ys, *remote):
+    greet(counts)
     total[...] = jnp.zeros_like(total)
 
     def body(step, carry):
         lanes = pl.ds(pl.multiple_of(step * chunk, chunk), chunk)
         vel, aff, ratio = gather_chunk(
-            base[0, :, lanes], offset[0, :, lanes], vol[:, lanes], sizes, wide, tab, result, tables
+            base[0, :, lanes], offset[0, :, lanes], vol[:, lanes], sizes, before, seen, result,
+            (xw, xs, yw, ys),
         )
         vol_out[:, lanes] = ratio
         scatter_chunk(
-            base[1, :, lanes], offset[1, :, lanes], vel, aff, ratio, sizes, tab, right, tables, total
+            base[1, :, lanes], offset[1, :, lanes], vel, aff, ratio, sizes, tab.at[step],
+            right.at[step], (xw, xs, yw, ys), total,
         )
         return carry
 
     lax.fori_loop(0, vol.shape[1] // chunk, body, 0)
-    edge = margins.shape[0]
-    margins[...] = total[0:edge].astype(BF16)
-    core[...] = total[edge:]
-
-
-def last_kernel(sizes, chunk, capacity, counts, base, offset, vol, wide, direction, own, buckets, tab, result, state, slots, *tables):
+    exchange(sizes, counts, mask, place_in, take_out, wide, tab, right, total, *remote)
+
+
+def last_kernel(sizes, chunk, capacity, counts, base, offset, vol, wide, direction, out, tab, result, state, slots, xw, xs, yw, ys, buckets, got, sends, recvs):
+    greet(counts)
+    tables = (xw, xs, yw, ys)
     size_x, size_y, _ = sizes
     count_x, count_y = counts
     index_x = lax.axis_index("gx")
@@ -252,7 +256,7 @@
         for k in range(9):
             state[6 + k : 7 + k, lanes] = aff[k]
         state[15:16, lanes] = ratio
-        own[:, lanes] = jnp.where(moving == 4, state[:, lanes], 0.0)
+        out[:, lanes] = jnp.where(moving == 4, state[:, lanes], 0.0)
         return carry
 
     lax.fori_loop(0, rows // chunk, body, 0)
@@ -287,6 +291,7 @@
         chosen = jnp.where(chosen, 1.0, 0.0).astype(BF16)
         packed = lax.dot_general(split, chosen, NT, preferred_element_type=F32)
         buckets[k] = packed[0:16] + packed[16:32] + packed[32:48]
+    migrate(counts, buckets, out, got, sends, recvs)
 
 
 def neighbour(counts, dx, dy):
@@ -307,6 +312,9 @@
                 barrier, inc=1, device_id=where, device_id_type=pl.DeviceIdType.MESH
             )
 
+
+def await_peers(counts):
+    barrier = pltpu.get_barrier_semaphore()
     peers = 0
     for dx, dy in BLOCKS:
         exists, _ = neighbour(counts, dx, dy)
@@ -314,13 +322,13 @@
     pl.semaphore_wait(barrier, peers)
 
 
-def transfers(counts, sign, views, source, target, send_sems, recv_sems):
+def transfers(counts, sign, source, target, send_sems, recv_sems):
     copies = []
     for k, (dx, dy) in enumerate(BLOCKS):
         exists, where = neighbour(counts, sign * dx, sign * dy)
         copy = pltpu.make_async_remote_copy(
-            src_ref=views(source, k),
-            dst_ref=views(target, k),
+            src_ref=source(k),
+            dst_ref=target(k),
             send_sem=send_sems.at[k],
             recv_sem=recv_sems.at[k],
             device_id=where,
@@ -331,69 +339,123 @@
     return copies
 
 
-def start_all(copies, views, target):
+def start_all(copies, target):
     for exists, _, copy in copies:
         pl.when(exists)(copy.start)
     for k, (_, comes, _) in enumerate(copies):
 
         @pl.when(jnp.logical_not(comes))
         def _():
-            view = views(target, k)
+            view = target(k)
             view[...] = jnp.zeros(view.shape, view.dtype)
 
 
 def wait_all(copies):
-    for exists, comes, copy in copies:
+    for _, comes, copy in copies:
         pl.when(comes)(copy.wait_recv)
-    for exists, comes, copy in copies:
+    for exists, _, copy in copies:
         pl.when(exists)(copy.wait_send)
 
 
-def grid_kernel(sizes, counts, core, margins, mask, place_in, take_out, wide, got, sent, halo, speed, sends, recvs, sends_b, recvs_b):
+def pack_corners(value, channels, depth, spread):
+    for k in range(4):
+        for c in range(channels):
+            spread[k * CORNER_ROWS + 4 * c : k * CORNER_ROWS + 4 * c + 4, :] = value(
+                slice(k * CORNER_ROWS, k * CORNER_ROWS + 4), slice(c * depth, (c + 1) * depth)
+            )
+
+
+def unpack_corners(spread, channels, depth, square):
+    square[...] = jnp.zeros_like(square)
+    for k in range(4):
+        for c in range(channels):
+            square[
+                k * CORNER_ROWS : k * CORNER_ROWS + 4, c * depth : (c + 1) * depth
+            ] = spread[k * CORNER_ROWS + 4 * c : k * CORNER_ROWS + 4 * c + 4, :]
+
+
+def exchange(sizes, counts, mask, place_in, take_out, wide, tab, right, total, margins, corners, got, got_corners, sent, sent_corners, halo, halo_corners, spread, square, speed, drawn, sends, recvs, sends_b, recvs_b):
     size_x, size_y, depth = sizes
     places, edge = block_rows(size_x, size_y)
-
-    def views(ref, k):
-        return ref.at[pl.ds(places[k][0], places[k][1])]
-
-    greet(counts)
-    copies = transfers(counts, 1, views, margins, got, sends, recvs)
-    start_all(copies, views, got)
+    inner = places[4][0]
+
+    def views(sides, tiles):
+        def view(k):
+            if k < 4:
+                return sides.at[pl.ds(places[k][0], places[k][1])]
+            return tiles.at[pl.ds((k - 4) * CORNER_ROWS, CORNER_ROWS)]
+
+        return view
+
+    margins[...] = total[0:inner].astype(BF16)
+
+    def corner_of(rows, lanes):
+        return total[inner + rows.start : inner + rows.stop, lanes]
+
+    pack_corners(corner_of, 4, depth, spread)
+    corners[...] = spread[...].astype(BF16)
+    await_peers(counts)
+    arriving = views(got, got_corners)
+    copies = transfers(counts, 1, views(margins, corners), arriving, sends, recvs)
+    start_all(copies, arriving)
+
+    def body(step, carry):
+        total[edge:] += lax.dot_general(
+            tab[step, edge:], right[step], NT, preferred_element_type=F32
+        )
+        return carry
+
+    lax.fori_loop(0, tab.shape[0], body, 0)
     wait_all(copies)
-    total = core[...] + jnp.dot(place_in[...], got[...], preferred_element_type=F32)
-    mass = jnp.maximum(total[:, 0:depth], MASS_FLOOR)
+    spread[...] = got_corners[...].astype(F32)
+    unpack_corners(spread, 4, depth, square)
+    received = jnp.concatenate([got[...], square[...].astype(BF16)], 0)
+    full = total[edge:] + jnp.dot(place_in[...], received, preferred_element_type=F32)
+    mass = jnp.maximum(full[:, 0:depth], MASS_FLOOR)
     keep = (1 - mask[...]).astype(F32)
     for axis in range(3):
-        value = total[:, (axis + 1) * depth : (axis + 2) * depth] / mass
+        value = full[:, (axis + 1) * depth : (axis + 2) * depth] / mass
         if axis == 2:
             value = value - TIME_STEP * GRAVITY
         speed[:, axis * depth : (axis + 1) * depth] = (value * keep).astype(BF16)
-    sent[...] = jnp.dot(take_out[...], speed[...], preferred_element_type=F32).astype(BF16)
-    copies = transfers(counts, -1, views, sent, halo, sends_b, recvs_b)
-    start_all(copies, views, halo)
+    drawn[...] = jnp.dot(take_out[...], speed[...], preferred_element_type=F32)
+    sent[...] = drawn[0:inner].astype(BF16)
+
+    def drawn_corner(rows, lanes):
+        return drawn[inner + rows.start : inner + rows.stop, lanes]
+
+    pack_corners(drawn_corner, 3, depth, spread)
+    sent_corners[...] = spread[...].astype(BF16)
+    arriving = views(halo, halo_corners)
+    copies = transfers(counts, -1, views(sent, sent_corners), arriving, sends_b, recvs_b)
+    start_all(copies, arriving)
     for axis in range(3):
         lanes = slice(axis * depth, (axis + 1) * depth)
         wide[lanes, edge:] = speed[:, lanes].astype(F32).T.astype(BF16)
     wait_all(copies)
+    spread[...] = halo_corners[...].astype(F32)
+    unpack_corners(spread, 3, depth, square)
     for axis in range(3):
         lanes = slice(axis * depth, (axis + 1) * depth)
-        wide[lanes, 0:edge] = halo[:, lanes].astype(F32).T.astype(BF16)
-
-
-def migrate_kernel(counts, buckets, out, got, sends, recvs):
+        outer = jnp.concatenate([halo[:, lanes].astype(F32), square[:, lanes]], 0)
+        wide[lanes, 0:edge] = outer.T.astype(BF16)
+
+
+def migrate(counts, buckets, out, got, sends, recvs):
     capacity = buckets.shape[2]
+    rows = out.shape[1] - 8 * capacity
     order = [0, 1, 2, 3, 5, 6, 7, 8]
     slot_of = [order.index(3 * (dx + 1) + dy + 1) for dx, dy in BLOCKS]
 
-    def views(ref, k):
-        return ref.at[slot_of[k]]
-
-    greet(counts)
-    copies = transfers(counts, 1, views, buckets, got, sends, recvs)
-    start_all(copies, views, got)
+    def views(ref):
+        return lambda k: ref.at[slot_of[k]]
+
+    await_peers(counts)
+    copies = transfers(counts, 1, views(buckets), views(got), sends, recvs)
+    start_all(copies, views(got))
     wait_all(copies)
     for k in range(8):
-        out[:, k * capacity : (k + 1) * capacity] = got[k]
+        out[:, rows + k * capacity : rows + (k + 1) * capacity] = got[k]
 
 
 def vmem(count):
@@ -417,80 +479,67 @@
     take_out = jnp.asarray(choose, BF16)
     place_in = jnp.asarray(choose.T, BF16)
 
-    tab = pltpu.VMEM((all_rows, 3 * chunk), BF16)
-    right = pltpu.VMEM((4 * depth, 3 * chunk), BF16)
+    inner = edge - 4 * CORNER_ROWS
+    steps = rows // chunk
+    seen = pltpu.VMEM((all_rows, 3 * chunk), BF16)
     result = pltpu.VMEM((3 * depth, 3 * chunk), F32)
-    total = pltpu.VMEM((all_rows, 4 * depth), F32)
     tables = [pltpu.VMEM((size_x + 8, chunk), F32)] * 2 + [pltpu.VMEM((size_y + 8, chunk), F32)] * 2
-    grid_out = [
-        jax.ShapeDtypeStruct((cells, 4 * depth), F32),
-        jax.ShapeDtypeStruct((edge, 4 * depth), BF16),
-    ]
-    params = pltpu.CompilerParams(vmem_limit_bytes=56 * 1024 * 1024)
-
-    core, margins = pl.pallas_call(
-        functools.partial(first_kernel, sizes, chunk),
-        out_shape=grid_out,
+    spread = [
+        pltpu.VMEM((steps, all_rows, 3 * chunk), BF16),
+        pltpu.VMEM((steps, 4 * depth, 3 * chunk), BF16),
+        pltpu.VMEM((all_rows, 4 * depth), F32),
+    ] + tables
+    remote = [
+        pltpu.VMEM((inner, 4 * depth), BF16),
+        pltpu.VMEM((4 * CORNER_ROWS, depth), BF16),
+        pltpu.VMEM((inner, 4 * depth), BF16),
+        pltpu.VMEM((4 * CORNER_ROWS, depth), BF16),
+        pltpu.VMEM((inner, 3 * depth), BF16),
+        pltpu.VMEM((4 * CORNER_ROWS, depth), BF16),
+        pltpu.VMEM((inner, 3 * depth), BF16),
+        pltpu.VMEM((4 * CORNER_ROWS, depth), BF16),
+        pltpu.VMEM((4 * CORNER_ROWS, depth), F32),
+        pltpu.VMEM((4 * CORNER_ROWS, 4 * depth), F32),
+        pltpu.VMEM((cells, 3 * depth), BF16),
+        pltpu.VMEM((edge, 3 * depth), F32),
+    ] + [pltpu.SemaphoreType.DMA((8,))] * 4
+    wide_out = jax.ShapeDtypeStruct((3 * depth, all_rows), BF16)
+
+    def params(number):
+        return pltpu.CompilerParams(
+            collective_id=number, has_side_effects=True, vmem_limit_bytes=56 * 1024 * 1024
+        )
+
+    wide = pl.pallas_call(
+        functools.partial(first_kernel, sizes, counts, chunk),
+        out_shape=wide_out,
+        in_specs=vmem(8),
+        out_specs=vmem(1)[0],
+        scratch_shapes=spread + remote,
+        compiler_params=params(0),
+        name="scatter",
+    )(base, offset, velocity, affine, volume, mask, place_in, take_out)
+    wide, volume = pl.pallas_call(
+        functools.partial(middle_kernel, sizes, counts, chunk),
+        out_shape=[wide_out, jax.ShapeDtypeStruct((1, rows), F32)],
+        in_specs=vmem(7),
+        out_specs=vmem(2),
+        scratch_shapes=[seen, result] + spread + remote,
+        compiler_params=params(1),
+        name="gather_scatter",
+    )(base, offset, volume, wide, mask, place_in, take_out)
+    return pl.pallas_call(
+        functools.partial(last_kernel, sizes, chunk, capacity, counts),
+        out_shape=jax.ShapeDtypeStruct((16, rows + 8 * capacity), F32),
         in_specs=vmem(5),
-        out_specs=vmem(2),
-        scratch_shapes=[tab, right, total] + tables,
-        compiler_params=params,
-        name="scatter",
-    )(base, offset, velocity, affine, volume)
-
-    def exchange(core, margins):
-        return pl.pallas_call(
-            functools.partial(grid_kernel, sizes, counts),
-            out_shape=jax.ShapeDtypeStruct((3 * depth, all_rows), BF16),
-            in_specs=vmem(5),
-            out_specs=vmem(1)[0],
-            scratch_shapes=[
-                pltpu.VMEM((edge, 4 * depth), BF16),
-                pltpu.VMEM((edge, 3 * depth), BF16),
-                pltpu.VMEM((edge, 3 * depth), BF16),
-                pltpu.VMEM((cells, 3 * depth), BF16),
-            ]
-            + [pltpu.SemaphoreType.DMA((8,))] * 4,
-            compiler_params=pltpu.CompilerParams(
-                collective_id=0, has_side_effects=True, vmem_limit_bytes=56 * 1024 * 1024
-            ),
-            name="exchange",
-        )(core, margins, mask, place_in, take_out)
-
-    wide = exchange(core, margins)
-    core, margins, volume = pl.pallas_call(
-        functools.partial(middle_kernel, sizes, chunk),
-        out_shape=grid_out + [jax.ShapeDtypeStruct((1, rows), F32)],
-        in_specs=vmem(4),
-        out_specs=vmem(3),
-        scratch_shapes=[tab, result, right, total] + tables,
-        compiler_params=params,
-        name="gather_scatter",
-    )(base, offset, volume, wide)
-    wide = exchange(core, margins)
-    own, buckets = pl.pallas_call(
-        functools.partial(last_kernel, sizes, chunk, capacity, counts),
-        out_shape=[
-            jax.ShapeDtypeStruct((16, rows), F32),
-            jax.ShapeDtypeStruct((8, 16, capacity), F32),
-        ],
-        in_specs=vmem(5),
-        out_specs=vmem(2),
-        scratch_shapes=[tab, result, pltpu.VMEM((16, rows), F32), pltpu.VMEM((1, rows), jnp.int32)]
-        + tables,
-        compiler_params=params,
+        out_specs=vmem(1)[0],
+        scratch_shapes=[seen, result, pltpu.VMEM((16, rows), F32), pltpu.VMEM((1, rows), jnp.int32)]
+        + tables
+        + [pltpu.VMEM((8, 16, capacity), F32)] * 2
+        + [pltpu.SemaphoreType.DMA((8,))] * 2,
+        compiler_params=params(2),
         name="gather_pack",
     )(base, offset, volume, wide, direction)
-    arrived = pl.pallas_call(
-        functools.partial(migrate_kernel, counts),
-        out_shape=jax.ShapeDtypeStruct((16, 8 * capacity), F32),
-        in_specs=vmem(1),
-        out_specs=vmem(1)[0],
-        scratch_shapes=[pltpu.VMEM((8, 16, capacity), F32)] + [pltpu.SemaphoreType.DMA((8,))] * 2,
-        compiler_params=pltpu.CompilerParams(collective_id=1, has_side_effects=True),
-        name="migrate",
-    )(buckets)
-    return jnp.concatenate([own, arrived], 1)
 
 
 def solution(mesh):

time: 72.8 us -> 55.4 us (0.76)
  Pallas kernels: 68.7 us -> 51.4 us
  local copies, waits for them, and re-layouts: 2.12 us -> 3.74 us
  other arithmetic: 1.53 us -> 0 us
    pallas_call x5 -> x2, Pallas kernels: 60.2 us -> 38.3 us  [the longest x1 21.2 us: per_device(): pl.pallas_call(functools.partial(middle_kernel, sizes, counts, chunk), ou...]
    pallas_call x1, Pallas kernels: 8.49 us -> 13.1 us  [per_device(): pl.pallas_call(functools.partial(last_kernel, sizes, chunk, capacity, cou...]
    unnamed x6 -> x5, local copies, waits for them, and re-layouts: 2.12 us -> 3.74 us
    concatenate x1 -> x0, other arithmetic: 1.53 us -> none  [per_device(): return jnp.concatenate([own, arrived], 1)]
where the time goes in v1:
time: 55.4 us; the launch traced here: 55.1 us
  Pallas kernels  51.4 us (93%)
  local copies, waits for them, and re-layouts  3.74 us (7%)
    pallas_call x1, Pallas kernels, per_device(): pl.pallas_call(functools.partial(middle_kernel, sizes, counts, chunk), ou...  21.2 us
    pallas_call x1, Pallas kernels, per_device(): pl.pallas_call(functools.partial(first_kernel, sizes, counts, chunk), out...  17 us
    pallas_call x1, Pallas kernels, per_device(): pl.pallas_call(functools.partial(last_kernel, sizes, chunk, capacity, cou...  13.1 us
    unnamed x5, local copies, waits for them, and re-layouts  3.74 us

profile of v1, /device:TPU:0, one launch (start us, length us, event | category | flops | bytes accessed | tf_op | source)
XLA Modules:
  0.0 55.1 jit_solution(7294979098443377070)
XLA Ops:
  0.0 0.0 copy-start
  0.0 1.5 %copy.14.base = s32[2,3,2048]{2,1,0:T(4,128)} copy(s32[2,3,2048]{2,0,1:T(2,128)} %param.9) | data formatting | bytes 98304 | tf_op args[0]
  1.5 0.0 copy-done
  1.5 0.7 %copy.15.offset = f32[2,3,2048]{2,1,0:T(4,128)} copy(f32[2,3,2048]{2,0,1:T(2,128)S(1)} %copy-done) | data formatting | bytes 98304 | tf_op args[1]
  2.1 17.0 %scatter.1.before = bf16[384,768]{1,0:T(8,128)(2,1)} custom-call(s32[2,3,2048]{2,1,0:T(4,128)} %copy.14.base, f32[2,3,2048]{2,1,0:T(4,128)} %copy.15.offset, f32[3,2048]{1,0:T(4,128)} %vel.1, f32[9,2048]{1,0:T(8,128)} %aff.1, f32[1,2048]{1,0:T(1,128)} %bitcast.5, s32[512,128]{1,0:T(8,128)} %bitcast.3, bf16[512,256]{1,0:T(8,128)(2,1)} %constant.5.clone.place_in, ...), custom_call_target="tpu_custom_call" | custom-call | tf_op jit(solution)/shard_map/scatter/pallas_call | solution.py:513
  19.2 21.2 %gather_scatter.1 = (bf16[384,768]{1,0:T(8,128)(2,1)}, f32[1,2048]{1,0:T(1,128)}) custom-call(s32[2,3,2048]{2,1,0:T(4,128)} %copy.14.base, f32[2,3,2048]{2,1,0:T(4,128)} %copy.15.offset, f32[1,2048]{1,0:T(1,128)} %bitcast.6, bf16[384,768]{1,0:T(8,128)(2,1)} %scatter.1.before, s32[512,128]{1,0:T(8,128)} %bitcast.4, bf16[512,256]{1,0:T(8,128)(2,1)} %constant.5.clone.place_in, ...), custom_call_target="tpu_custom_call" | custom-call | tf_op jit(solution)/shard_map/gather_scatter/pallas_call | solution.py:522
  40.4 13.1 %gather_pack.1 = f32[16,3072]{1,0:T(8,128)} custom-call(s32[2,3,2048]{2,1,0:T(4,128)} %copy.14.base, f32[2,3,2048]{2,1,0:T(4,128)} %copy.15.offset, f32[1,2048]{1,0:T(1,128)} %get-tuple-element.7.vol, bf16[384,768]{1,0:T(8,128)(2,1)} %get-tuple-element.8.wide, s32[1,2048]{1,0:T(1,128)} %bitcast.7), custom_call_target="tpu_custom_call" | custom-call | tf_op jit(solution)/shard_map/gather_pack/pallas_call | solution.py:531
  53.5 1.6 %copy.17 = f32[16,3072]{1,0:T(8,128)} copy(f32[16,3072]{1,0:T(8,128)} %gather_pack.1) | data formatting | bytes 393216
Async XLA Ops:
  0.0 1.5 %copy-start = (f32[2,3,2048]{2,0,1:T(2,128)S(1)}, f32[2,3,2048]{2,0,1:T(2,128)}, u32[]{:S(2)}) copy-start(f32[2,3,2048]{2,0,1:T(2,128)} %param.10) | copy-start | bytes 147460

commit v2 on v1

--- a/solution.py
+++ b/solution.py
@@ -185,7 +185,7 @@
     def body(step, carry):
         lanes = pl.ds(pl.multiple_of(step * chunk, chunk), chunk)
         scatter_chunk(
-            base[0, :, lanes], offset[0, :, lanes], take_rows(vel, lanes, 3),
+            base[:, 0, lanes], offset[:, 0, lanes], take_rows(vel, lanes, 3),
             take_rows(aff, lanes, 9), vol[:, lanes], sizes, tab.at[step], right.at[step],
             (xw, xs, yw, ys), total,
         )
@@ -202,12 +202,12 @@
     def body(step, carry):
         lanes = pl.ds(pl.multiple_of(step * chunk, chunk), chunk)
         vel, aff, ratio = gather_chunk(
-            base[0, :, lanes], offset[0, :, lanes], vol[:, lanes], sizes, before, seen, result,
+            base[:, 0, lanes], offset[:, 0, lanes], vol[:, lanes], sizes, before, seen, result,
             (xw, xs, yw, ys),
         )
         vol_out[:, lanes] = ratio
         scatter_chunk(
-            base[1, :, lanes], offset[1, :, lanes], vel, aff, ratio, sizes, tab.at[step],
+            base[:, 1, lanes], offset[:, 1, lanes], vel, aff, ratio, sizes, tab.at[step],
             right.at[step], (xw, xs, yw, ys), total,
         )
         return carry
@@ -239,8 +239,8 @@
 
     def body(step, carry):
         lanes = pl.ds(pl.multiple_of(step * chunk, chunk), chunk)
-        bases = base[1, :, lanes]
-        offsets = offset[1, :, lanes]
+        bases = base[:, 1, lanes]
+        offsets = offset[:, 1, lanes]
         vel, aff, ratio = gather_chunk(
             bases, offsets, vol[:, lanes], sizes, wide, tab, result, tables
         )
@@ -471,6 +471,8 @@
     _, edge = block_rows(size_x, size_y)
     cells = size_x * size_y
     all_rows = edge + cells
+    base = jnp.swapaxes(base, 0, 1)
+    offset = jnp.swapaxes(offset, 0, 1)
     volume = volume.reshape(1, rows)
     direction = direction.reshape(1, rows)
     mask = node_mask.reshape(cells, depth)

time: 55.4 us -> 52.5 us (0.948)
  local copies, waits for them, and re-layouts: 3.74 us -> 1.62 us
  Pallas kernels: 51.4 us -> 50.7 us
    unnamed x5 -> x1, local copies, waits for them, and re-layouts: 3.74 us -> 1.62 us
    pallas_call x1, Pallas kernels: 21.2 us -> 20.7 us  [per_device(): pl.pallas_call(functools.partial(middle_kernel, sizes, counts, chunk), ou...]
where the time goes in v2:
time: 52.5 us; the launch traced here: 52.3 us
  Pallas kernels  50.7 us (97%)
  local copies, waits for them, and re-layouts  1.62 us (3%)
    pallas_call x1, Pallas kernels, per_device(): pl.pallas_call(functools.partial(middle_kernel, sizes, counts, chunk), ou...  20.7 us
    pallas_call x1, Pallas kernels, per_device(): pl.pallas_call(functools.partial(first_kernel, sizes, counts, chunk), out...  17 us
    pallas_call x1, Pallas kernels, per_device(): pl.pallas_call(functools.partial(last_kernel, sizes, chunk, capacity, cou...  13 us
    unnamed x1, local copies, waits for them, and re-layouts  1.62 us

profile of v2, /device:TPU:0, one launch (start us, length us, event | category | flops | bytes accessed | tf_op | source)
XLA Modules:
  0.0 52.3 jit_solution(9166543919780105284)
XLA Ops:
  0.0 17.0 %scatter.1.before = bf16[384,768]{1,0:T(8,128)(2,1)} custom-call(s32[3,2,2048]{2,1,0:T(2,128)} %bitcast.7, f32[3,2,2048]{2,1,0:T(2,128)} %bitcast.10, f32[3,2048]{1,0:T(4,128)} %vel.1, f32[9,2048]{1,0:T(8,128)} %aff.1, f32[1,2048]{1,0:T(1,128)} %bitcast.13, s32[512,128]{1,0:T(8,128)} %bitcast.5, bf16[512,256]{1,0:T(8,128)(2,1)} %constant.5.clone.place_in, ...), custom_call_target="tpu_custom_call" | custom-call | tf_op jit(solution)/shard_map/scatter/pallas_call | solution.py:515
  17.0 20.7 %gather_scatter.1 = (bf16[384,768]{1,0:T(8,128)(2,1)}, f32[1,2048]{1,0:T(1,128)}) custom-call(s32[3,2,2048]{2,1,0:T(2,128)} %bitcast.8, f32[3,2,2048]{2,1,0:T(2,128)} %bitcast.11, f32[1,2048]{1,0:T(1,128)} %bitcast.14, bf16[384,768]{1,0:T(8,128)(2,1)} %scatter.1.before, s32[512,128]{1,0:T(8,128)} %bitcast.6, bf16[512,256]{1,0:T(8,128)(2,1)} %constant.5.clone.place_in, ...), custom_call_target="tpu_custom_call" | custom-call | tf_op jit(solution)/shard_map/gather_scatter/pallas_call | solution.py:524
  37.7 13.0 %gather_pack.1 = f32[16,3072]{1,0:T(8,128)} custom-call(s32[3,2,2048]{2,1,0:T(2,128)} %bitcast.9, f32[3,2,2048]{2,1,0:T(2,128)} %bitcast.12, f32[1,2048]{1,0:T(1,128)} %get-tuple-element.7.vol, bf16[384,768]{1,0:T(8,128)(2,1)} %get-tuple-element.8.wide, s32[1,2048]{1,0:T(1,128)} %bitcast.15), custom_call_target="tpu_custom_call" | custom-call | tf_op jit(solution)/shard_map/gather_pack/pallas_call | solution.py:533
  50.7 1.6 %copy.11 = f32[16,3072]{1,0:T(8,128)} copy(f32[16,3072]{1,0:T(8,128)} %gather_pack.1) | data formatting | bytes 393216
